TPU v7x, 512 devices: a whole 4x4x16 slice. The times are simulated.
512 devices in a mesh: fsdp: 8 (over y, core), trow: 16 (over x, z_hi), tcol: 4 (over z_lo).
Axes of the slice: x: 4, y: 4, z: 16 (z_hi: 4, z_lo: 4; z = z_hi * 4 + z_lo), core: 2. Of those that a mesh axis runs over, the one named last changes fastest.
Arguments:
- tokens: bfloat16 [2048, 4096], P('fsdp', 'tcol'), may hold values from -100 to 100
- w_up: bfloat16 [4096, 16384], P('tcol', ('fsdp', 'trow')), may hold values from -0.1875 to 0.1875
- w_down: bfloat16 [16384, 4096], P(('fsdp', 'trow'), 'tcol'), may hold values from -0.046875 to 0.046875
- cotangent: bfloat16 [2048, 4096], P('fsdp', 'tcol'), may hold values from -6 to 6
Outputs:
- mixed: bfloat16 [2048, 4096], P('fsdp', 'tcol')
- input_gradient: bfloat16 [2048, 4096], P('fsdp', 'tcol')
- grad_up: bfloat16 [4096, 16384], P('tcol', ('fsdp', 'trow'))
- grad_down: bfloat16 [16384, 4096], P(('fsdp', 'trow'), 'tcol')
All inputs are finite; a program needn't handle non-finite values.
Results may differ from a plain program's by a relative error of at most 0.02.
Values may be sent and summed in bfloat16 or wider, within the bound.
A program may use at most 64 MiB of HBM per device.

v0:
```python
import jax
import jax.numpy as jnp
from jax import lax
from jax.experimental import pallas as pl
from jax.experimental.pallas import tpu as pltpu
from jax.sharding import PartitionSpec as P

BF = jnp.bfloat16
F32 = jnp.float32
OWN, PREV, NEXT, FAR = 0, 1, 2, 3


def gelu_value(pre):
    phi = 0.5 * (1.0 + lax.erf(pre * 0.7071067811865476))
    return pre * phi


def gelu_slope(pre):
    phi = 0.5 * (1.0 + lax.erf(pre * 0.7071067811865476))
    return phi + pre * jnp.exp(-0.5 * pre * pre) * 0.3989422804014327


def dot(left, right, left_dim, right_dim):
    return lax.dot_general(
        left, right, (((left_dim,), (right_dim,)), ((), ())), preferred_element_type=F32
    )


class Wire:
    def __init__(self, send_sems, recv_sems):
        self.send_sems, self.recv_sems = send_sems, recv_sems
        self.count = 0
        self.sent = []

    def slot(self):
        self.count += 1
        return self.count - 1

    def copy(self, src, dst, device, slot):
        return pltpu.make_async_remote_copy(
            src_ref=src,
            dst_ref=dst,
            send_sem=self.send_sems.at[slot],
            recv_sem=self.recv_sems.at[slot],
            device_id=device,
            device_id_type=pl.DeviceIdType.MESH,
        )

    def send(self, src, dst, device, slot=None, when=None):
        slot = self.slot() if slot is None else slot
        made = self.copy(src, dst, device, slot)
        if when is None:
            made.start()
        else:
            pl.when(when)(made.start)
        self.sent.append((made, when))
        return made

    def drain(self):
        for made, when in self.sent:
            if when is None:
                made.wait_send()
            else:
                pl.when(when)(made.wait_send)


class RingSum:
    def __init__(self, wire, plus, minus, block, half, bufs):
        self.w, self.plus, self.minus, self.block, self.half = wire, plus, minus, block, half
        self.r1a, self.r1b, self.r2p, self.r2m, self.ga, self.gb = bufs

    def start(self):
        self.start_far()
        self.start_near()

    def start_far(self):
        w = self.w
        self.c1 = w.send(self.block(2, 0), self.r1a, self.plus)
        self.c2 = w.send(self.block(2, 1), self.r1b, self.minus)

    def start_near(self):
        w, half = self.w, self.half
        self.c3 = w.send(self.block(1, 1), half(self.r2p, 1), self.plus)
        self.c4 = w.send(self.block(-1, 0), half(self.r2m, 0), self.minus)

    def mid(self):
        w, half = self.w, self.half
        self.c1.wait_recv()
        self.ga[...] = (self.block(1, 0)[...].astype(F32) + self.r1a[...].astype(F32)).astype(BF)
        self.c5 = w.send(self.ga, half(self.r2p, 0), self.plus)
        self.c2.wait_recv()
        self.gb[...] = (self.block(-1, 1)[...].astype(F32) + self.r1b[...].astype(F32)).astype(BF)
        self.c6 = w.send(self.gb, half(self.r2m, 1), self.minus)

    def end(self, own):
        for c in (self.c3, self.c4, self.c5, self.c6):
            c.wait_recv()
        return own + self.r2p[...].astype(F32) + self.r2m[...].astype(F32)


class RingCopy:
    def __init__(self, wire, plus, minus, own, at_plus, at_minus, near, far):
        self.w, self.plus, self.minus = wire, plus, minus
        self.own, self.at_plus, self.at_minus, self.near, self.far = own, at_plus, at_minus, near, far

    def start(self):
        w = self.w
        self.p0 = w.send(self.own(0), self.at_plus(0), self.plus)
        self.m1 = w.send(self.own(1), self.at_minus(1), self.minus)
        self.p1 = w.send(self.own(1), self.at_plus(1), self.plus)
        self.m0 = w.send(self.own(0), self.at_minus(0), self.minus)

    def mid(self):
        w = self.w
        self.p0.wait_recv()
        self.f0 = w.send(self.near(-1, 0), self.far(-1, 0), self.plus)
        self.m1.wait_recv()
        self.f1 = w.send(self.near(1, 1), self.far(1, 1), self.minus)

    def near_end(self):
        self.p1.wait_recv()
        self.m0.wait_recv()

    def far_end(self):
        self.f0.wait_recv()
        self.f1.wait_recv()


SCRATCH = dict(
    x=((512, 1024), BF),
    c=((512, 1024), BF),
    tk=((256, 1024), BF),
    wu=((1024, 512), BF),
    wd=((512, 1024), BF),
    sstat=((8, 256), F32),
    rstat=((3, 8, 256), F32),
    mean=((256, 128), F32),
    rstd=((256, 128), F32),
    part=((2, 512, 512), BF),
    pa=((2, 4, 256, 128), BF),
    pb=((2, 4, 256, 128), BF),
    pf=((2, 4, 256, 128), BF),
    pg=((2, 4, 256, 128), BF),
    pre=((4, 256, 128), F32),
    hid=((2, 512, 512), BF),
    bs=((2, 256, 1024), BF),
    br=((2, 256, 1024), BF),
    xacc=((2, 256, 1024), F32),
    xown=((2, 4, 16, 1024), F32),
    xs=((2, 4, 4, 16, 1024), BF),
    x1a=((2, 4, 16, 512), BF),
    x1b=((2, 4, 16, 512), BF),
    x2p=((2, 4, 16, 1024), BF),
    x2m=((2, 4, 16, 1024), BF),
    xga=((2, 4, 16, 512), BF),
    xgb=((2, 4, 16, 512), BF),
    zs=((2, 4, 16, 1024), BF),
    z1a=((2, 16, 512), BF),
    z1b=((2, 16, 512), BF),
    z2p=((2, 16, 1024), BF),
    z2m=((2, 16, 1024), BF),
    zga=((2, 16, 512), BF),
    zgb=((2, 16, 512), BF),
    fin=((2, 256, 1024), BF),
    ts=((1, 128), F32),
    tr=((15, 1, 128), F32),
    gdp=((512, 1024), BF),
    gdo=((128, 1024), F32),
    gd1a=((64, 1024), BF),
    gd1b=((64, 1024), BF),
    gd2p=((128, 1024), BF),
    gd2m=((128, 1024), BF),
    gdga=((64, 1024), BF),
    gdgb=((64, 1024), BF),
    gdout=((128, 1024), BF),
    gup=((1024, 512), BF),
    guo=((1024, 128), F32),
    gu1a=((512, 128), BF),
    gu1b=((512, 128), BF),
    gu2p=((1024, 128), BF),
    gu2m=((1024, 128), BF),
    guga=((512, 128), BF),
    gugb=((512, 128), BF),
    guout=((1024, 128), BF),
)
N_SEMS = 224


def rows_of(index, size):
    return pl.ds(pl.multiple_of(index * size, size), size)


def kernel(tok_h, wu_h, wd_h, cot_h, mix_h, ing_h, gu_h, gd_h, *scratch):
    s = dict(zip(SCRATCH, scratch))
    send_sems, recv_sems, local_sems = scratch[len(SCRATCH) :]
    wire = Wire(send_sems, recv_sems)

    fsdp, trow, tcol = lax.axis_index("fsdp"), lax.axis_index("trow"), lax.axis_index("tcol")
    y, core = fsdp // 2, lax.rem(fsdp, 2)
    xx, zh = trow // 4, lax.rem(trow, 4)
    zl = tcol

    def at(dy=0, dcore=0, dx=0, dzh=0):
        return (
            lax.rem(y + dy, 4) * 2 + lax.rem(core + dcore, 2),
            lax.rem(xx + dx, 4) * 4 + lax.rem(zh + dzh, 4),
            tcol,
        )

    def at_zl(index):
        return (fsdp, trow, index)

    partner = at(dcore=1)
    y_plus, y_minus = at(dy=1), at(dy=3)
    x_plus, x_minus = at(dx=1), at(dx=3)
    right = zl // 2
    mate = zl + 1 - 2 * lax.rem(zl, 2)
    far_hub = 2 - right
    is_hub = jnp.logical_or(zl == 1, zl == 2)
    is_end = jnp.logical_or(zl == 0, zl == 3)

    barrier = pltpu.get_barrier_semaphore()
    others = [partner, y_plus, y_minus, x_plus, x_minus]
    for dz in range(4):
        for dl in range(4):
            if dz or dl:
                fs, tr, _ = at(dzh=dz)
                others.append((fs, tr, lax.rem(zl + dl, 4)))
    loads = [
        pltpu.make_async_copy(src, dst, local_sems.at[i])
        for i, (src, dst) in enumerate(
            (
                (tok_h, s["tk"]),
                (wu_h, s["wu"].at[:, 0:128]),
                (wd_h, s["wd"].at[0:128]),
                (cot_h, s["c"].at[0:256]),
            )
        )
    ]
    for load in loads:
        load.start()
    for other in others:
        pl.semaphore_signal(
            barrier, inc=1, device_id=other, device_id_type=pl.DeviceIdType.MESH
        )

    loads[0].wait()
    tok = s["tk"][...].astype(F32)
    sum_one = jnp.sum(tok, axis=1, keepdims=True)
    sum_two = jnp.sum(tok * tok, axis=1, keepdims=True)
    lane = lax.broadcasted_iota(jnp.int32, (256, 128), 1)
    both = jnp.where(lane == 0, sum_one, jnp.where(lane == 1, sum_two, 0.0))
    s["sstat"][...] = jnp.transpose(both)[0:8]
    for load in loads[1:]:
        load.wait()
    pl.semaphore_wait(barrier, len(others))

    def wu_at(pos, h):
        return s["wu"].at[h * 512 : (h + 1) * 512, pos * 128 : (pos + 1) * 128]

    def wd_at(pos, h):
        return s["wd"].at[pos * 128 + h * 64 : pos * 128 + (h + 1) * 64]

    def weights(view):
        return RingCopy(
            wire,
            y_plus,
            y_minus,
            own=lambda h: view(OWN, h),
            at_plus=lambda h: view(PREV, h),
            at_minus=lambda h: view(NEXT, h),
            near=lambda rel, h: view(PREV if rel < 0 else NEXT, h),
            far=lambda rel, h: view(FAR, h),
        )

    ups, downs = weights(wu_at), weights(wd_at)
    ups.start()
    stat_copies = [
        wire.send(s["sstat"], s["rstat"].at[k - 1], at_zl(lax.rem(zl + k, 4))) for k in (1, 2, 3)
    ]
    cot_copy = wire.send(s["c"].at[0:256], s["c"].at[256:512], partner)

    class Exchange:
        def __init__(self, which, pos, first, count):
            self.which, self.first, self.count = which, first, count
            self.lanes = slice(pos * 128, (pos + 1) * 128)
            self.i = (which, pos, slice(first, first + count))
            self.slots = [wire.slot() for _ in range(6)]

        def rows(self, side):
            return pl.ds(pl.multiple_of(side * 256 + self.first, 128), self.count)

        def part(self, side):
            return s["part"].at[self.which, self.rows(side), self.lanes]

        def back(self, side):
            return s["hid"].at[self.which, self.rows(side), self.lanes]

        def start(self):
            far, near = self.slots[0:2]
            to = at_zl(mate)
            self.far = wire.send(self.part(1 - right), s["pb"].at[self.i], to, far, is_end)
            self.near = wire.send(self.part(right), s["pa"].at[self.i], to, near, is_end)

        def mid(self):
            made = wire.copy(s["pg"].at[self.i], s["pf"].at[self.i], at_zl(far_hub), self.slots[2])

            @pl.when(is_hub)
            def _():
                self.far.wait_recv()
                both = self.part(1 - right)[...].astype(F32) + s["pb"][self.i].astype(F32)
                s["pg"][self.i] = both.astype(BF)
                made.start()

            wire.sent.append((made, is_hub))
            self.cross = made

        def end(self, finish):
            mine = self.back(right)
            across = wire.copy(mine, mine, at_zl(far_hub), self.slots[3])
            down = wire.copy(mine, mine, at_zl(mate), self.slots[4])

            @pl.when(is_hub)
            def _():
                self.near.wait_recv()
                self.cross.wait_recv()
                total = self.part(right)[...].astype(F32) + s["pa"][self.i].astype(F32)
                total = total + s["pf"][self.i].astype(F32)
                s["hid"][self.which, self.rows(right), self.lanes] = finish(total, self.i)
                across.start()
                down.start()

            wire.sent += [(across, is_hub), (down, is_hub)]
            self.across, self.down = across, down

        def back_mid(self):
            theirs = self.back(1 - right)
            made = wire.copy(theirs, theirs, at_zl(mate), self.slots[5])

            @pl.when(is_hub)
            def _():
                self.across.wait_recv()
                made.start()

            wire.sent.append((made, is_hub))
            self.passed = made

        def back_end(self):
            @pl.when(is_end)
            def _():
                self.down.wait_recv()
                self.passed.wait_recv()

    def gelu_of(total, i):
        s["pre"][i[1:]] = total
        return gelu_value(total).astype(BF)

    def dpre_of(total, i):
        return (total * gelu_slope(s["pre"][i[1:]])).astype(BF)

    pres = [[Exchange(0, pos, 0, 256)] for pos in range(4)]
    dhs = [[Exchange(1, pos, 0, 256)] for pos in range(3)]
    dhs.append([Exchange(1, 3, 0, 128), Exchange(1, 3, 128, 128)])

    def every(exchanges, step, *args):
        for e in exchanges:
            getattr(e, step)(*args)

    def pre_part(first, last):
        lanes = slice(first * 128, last * 128)
        s["part"][0, :, lanes] = dot(s["x"][...], s["wu"][:, lanes], 1, 0).astype(BF)
        for pos in range(first, last):
            every(pres[pos], "start")

    def dh_part(first, last):
        lanes = slice(first * 128, last * 128)
        s["part"][1, :, lanes] = dot(s["c"][...], s["wd"][lanes], 1, 1).astype(BF)
        for pos in range(first, last):
            every(dhs[pos], "start")

    def pre_done(pos):
        every(pres[pos], "end", gelu_of)

    def dh_done(pos):
        every(dhs[pos], "end", dpre_of)

    cot_copy.wait_recv()
    dh_part(0, 1)

    for c in stat_copies:
        c.wait_recv()
    total = s["sstat"][...] + s["rstat"][0] + s["rstat"][1] + s["rstat"][2]
    total = jnp.transpose(jnp.concatenate([total, jnp.zeros((120, 256), F32)], axis=0))
    mean = total[:, 0:1] / 4096.0
    var = total[:, 1:2] / 4096.0 - mean * mean
    rstd = lax.rsqrt(var + 1e-05)
    s["mean"][...] = jnp.broadcast_to(mean, (256, 128))
    s["rstd"][...] = jnp.broadcast_to(rstd, (256, 128))
    s["x"][0:256] = ((s["tk"][...].astype(F32) - mean) * rstd).astype(BF)
    x_copy = wire.send(s["x"].at[0:256], s["x"].at[256:512], partner)
    ups.mid()
    downs.start()
    x_copy.wait_recv()
    pre_part(0, 1)
    every(dhs[0], "mid")
    ups.near_end()
    pre_part(1, 3)
    every(pres[0], "mid")
    ups.far_end()
    pre_part(3, 4)
    pre_done(0)
    dh_done(0)
    every(pres[1], "mid")
    every(pres[2], "mid")
    downs.mid()
    every(pres[3], "mid")
    every(pres[0], "back_mid")
    every(dhs[0], "back_mid")
    pre_done(1)
    downs.near_end()
    dh_part(1, 3)
    pre_done(2)
    every(pres[1], "back_mid")
    pre_done(3)
    downs.far_end()
    dh_part(3, 4)
    every(dhs[1], "mid")
    every(dhs[2], "mid")
    every(pres[2], "back_mid")
    every(dhs[3], "mid")
    every(pres[3], "back_mid")
    dh_done(1)
    dh_done(2)
    dh_done(3)

    def rows(rel_x, rel_z):
        first = lax.rem(xx + rel_x, 4) * 64 + lax.rem(zh + rel_z, 4) * 16
        return pl.ds(pl.multiple_of(first, 16), 16)

    mine = rows(0, 0)
    steps = (2, 1, 3, 0)
    chunks = (slice(0, 1), slice(1, 4))

    def out_part(o, product):
        s["bs"][o] = product(1).astype(BF)
        sent = []
        for rel in (2, 1, 3, 0):
            r = rows_of(lax.rem(xx + rel, 4), 64)
            sent.append(wire.send(s["bs"].at[o, r], s["br"].at[o, r], partner))
        s["xacc"][o] = product(0)
        return sent

    def over_x(o, k):
        which = pl.ds(chunks[k].start, chunks[k].stop - chunks[k].start)

        def block(rel, h):
            return s["xs"].at[o, which, rel % 4, :, h * 512 : (h + 1) * 512]

        def half(ref, h):
            return ref.at[:, :, h * 512 : (h + 1) * 512]

        names = ("x1a", "x1b", "x2p", "x2m", "xga", "xgb")
        return RingSum(wire, x_plus, x_minus, block, half, [s[n].at[o, which] for n in names])

    x_sums = [[over_x(o, k) for k in (0, 1)] for o in (0, 1)]

    def x_start(o, copies):
        for rel, copy in zip((2, 1, 3, 0), copies):
            copy.wait_recv()
            for k, chunk in enumerate(chunks):
                for i in range(chunk.start, chunk.stop):
                    r = rows(rel, steps[i])
                    value = s["xacc"][o, r] + s["br"][o, r].astype(F32)
                    if rel == 0:
                        s["xown"][o, i] = value
                    else:
                        s["xs"][o, i, rel] = value.astype(BF)
                if rel == 2:
                    x_sums[o][k].start_far()
            if rel == 3:
                x_sums[o][0].start_near()
                x_sums[o][1].start_near()

    def over_z(o):
        def block(rel, h):
            return s["zs"].at[o, rel % 4, :, h * 512 : (h + 1) * 512]

        def half(ref, h):
            return ref.at[:, h * 512 : (h + 1) * 512]

        names = ("z1a", "z1b", "z2p", "z2m", "zga", "zgb")
        return RingSum(wire, at(dzh=1), at(dzh=3), block, half, [s[n].at[o] for n in names])

    z_sums = [over_z(0), over_z(1)]

    def z_start(o, k):
        chunk = chunks[k]
        value = x_sums[o][k].end(s["xown"][o, chunk])
        s["xown"][o, chunk] = value
        for i in range(chunk.start, min(chunk.stop, 3)):
            s["zs"][o, steps[i]] = value[i - chunk.start].astype(BF)
        if k == 0:
            z_sums[o].start_far()
        else:
            z_sums[o].start_near()

    def z_done(o):
        return z_sums[o].end(s["xown"][o, 3])

    def back_z(o):
        def view(rel, h):
            return s["fin"].at[o, rows(0, rel % 4), h * 512 : (h + 1) * 512]

        spread = RingCopy(
            wire,
            at(dzh=1),
            at(dzh=3),
            own=lambda h: view(0, h),
            at_plus=lambda h: view(0, h),
            at_minus=lambda h: view(0, h),
            near=view,
            far=view,
        )
        spread.start()
        return spread

    def back_x(o, rel_z):
        def view(rel, h):
            return s["fin"].at[o, rows(rel % 4, rel_z % 4), h * 512 : (h + 1) * 512]

        return RingCopy(
            wire,
            x_plus,
            x_minus,
            own=lambda h: view(0, h),
            at_plus=lambda h: view(0, h),
            at_minus=lambda h: view(0, h),
            near=view,
            far=view,
        )

    def back_x_start(o, rel_z):
        spread = back_x(o, rel_z)
        spread.start()
        return spread

    pos_of = {1: NEXT, 2: FAR, -1: PREV}

    def gd_block(rel, h):
        first = pos_of[rel] * 128 + h * 64
        return s["gdp"].at[first : first + 64]

    def gu_block(rel, h):
        pos = pos_of[rel]
        return s["gup"].at[h * 512 : (h + 1) * 512, pos * 128 : (pos + 1) * 128]

    gd_names = ("gd1a", "gd1b", "gd2p", "gd2m", "gdga", "gdgb")
    gu_names = ("gu1a", "gu1b", "gu2p", "gu2m", "guga", "gugb")
    gd_sum = RingSum(
        wire, y_plus, y_minus, gd_block, lambda r, h: r.at[h * 64 : (h + 1) * 64],
        [s[n] for n in gd_names],
    )
    gu_sum = RingSum(
        wire, y_plus, y_minus, gu_block, lambda r, h: r.at[h * 512 : (h + 1) * 512],
        [s[n] for n in gu_names],
    )

    for pos in range(4):
        every(pres[pos], "back_end")
    branch_copy = out_part(
        0, lambda half: dot(s["hid"][0, half * 256 : (half + 1) * 256], s["wd"][...], 1, 0)
    )
    every(dhs[1], "back_mid")
    every(dhs[2], "back_mid")
    every(dhs[3], "back_mid")
    x_start(0, branch_copy)
    grad = dot(s["hid"][0], s["c"][...], 0, 0)
    s["gdo"][...] = grad[0:128]
    s["gdp"][128:512] = grad[128:512].astype(BF)
    gd_sum.start()
    for pos in range(4):
        every(dhs[pos], "back_end")

    dnorm_copy = out_part(
        1, lambda half: dot(s["hid"][1, half * 256 : (half + 1) * 256], s["wu"][...], 1, 1)
    )
    x_sums[0][0].mid()
    x_sums[0][1].mid()
    x_start(1, dnorm_copy)
    grad = dot(s["x"][...], s["hid"][1], 0, 0)
    s["guo"][...] = grad[:, 0:128]
    s["gup"][:, 128:512] = grad[:, 128:512].astype(BF)
    gu_sum.start()
    z_start(0, 0)
    z_start(0, 1)
    x_sums[1][0].mid()
    x_sums[1][1].mid()
    gd_sum.mid()
    z_start(1, 0)
    z_start(1, 1)

    lane = lax.broadcasted_iota(jnp.int32, (16, 128), 1)
    row = lax.broadcasted_iota(jnp.int32, (16, 128), 0)
    line = jnp.zeros((1, 128), F32)
    for i in range(4):
        part = s["xown"][1, i]
        r = rows(0, steps[i])
        xhat = (s["tk"][r, :].astype(F32) - s["mean"][r, 0:1]) * s["rstd"][r, 0:1]
        first = jnp.sum(part, axis=1, keepdims=True)
        second = jnp.sum(part * xhat, axis=1, keepdims=True)
        place = row + lax.rem(zh + steps[i], 4) * 16
        spot = jnp.where(lane == place, first, jnp.where(lane == place + 64, second, 0.0))
        line = line + jnp.sum(spot, axis=0, keepdims=True)
    s["ts"][...] = line
    moment_copies = []
    for dz in range(4):
        for dl in range(4):
            if dz or dl:
                fs, tr, _ = at(dzh=dz)
                other = (fs, tr, lax.rem(zl + dl, 4))
                moment_copies.append(wire.send(s["ts"], s["tr"].at[dz * 4 + dl - 1], other))
    z_sums[0].mid()
    gu_sum.mid()
    z_sums[1].mid()
    s["fin"][0, mine, :] = (s["tk"][mine, :].astype(F32) + z_done(0)).astype(BF)
    z_back0 = back_z(0)
    x_backs0 = [back_x_start(0, 0)]
    s["gdout"][...] = gd_sum.end(s["gdo"][...]).astype(BF)
    gd_out = pltpu.make_async_copy(s["gdout"], gd_h, local_sems.at[4])
    gd_out.start()

    dnorm = z_done(1)
    for c in moment_copies:
        c.wait_recv()
    line = s["ts"][...]
    for k in range(15):
        line = line + s["tr"][k]
    place = row + zh * 16
    moment_one = jnp.sum(jnp.where(lane == place, line, 0.0), axis=1, keepdims=True) / 4096.0
    moment_two = jnp.sum(jnp.where(lane == place + 64, line, 0.0), axis=1, keepdims=True) / 4096.0
    rstd = s["rstd"][mine, 0:1]
    xhat = (s["tk"][mine, :].astype(F32) - s["mean"][mine, 0:1]) * rstd
    grad = s["c"][mine, :].astype(F32) + rstd * (dnorm - moment_one - xhat * moment_two)
    s["fin"][1, mine, :] = grad.astype(BF)
    z_back1 = back_z(1)
    x_backs1 = [back_x_start(1, 0)]
    z_back0.mid()
    z_back0.near_end()
    x_backs0 += [back_x_start(0, 1), back_x_start(0, 3)]
    x_backs0[0].mid()
    x_backs1[0].mid()
    z_back1.mid()
    z_back1.near_end()
    x_backs1 += [back_x_start(1, 1), back_x_start(1, 3)]
    x_backs0[1].mid()
    x_backs0[2].mid()
    z_back0.far_end()
    x_backs0.append(back_x_start(0, 2))
    x_backs1[1].mid()
    x_backs1[2].mid()
    s["guout"][...] = gu_sum.end(s["guo"][...]).astype(BF)
    gu_out = pltpu.make_async_copy(s["guout"], gu_h, local_sems.at[5])
    gu_out.start()
    x_backs0[3].mid()
    z_back1.far_end()
    x_backs1.append(back_x_start(1, 2))
    for spread in x_backs0:
        spread.near_end()
        spread.far_end()
    mix_out = pltpu.make_async_copy(s["fin"].at[0], mix_h, local_sems.at[6])
    mix_out.start()
    x_backs1[3].mid()
    for spread in x_backs1:
        spread.near_end()
        spread.far_end()
    ing_out = pltpu.make_async_copy(s["fin"].at[1], ing_h, local_sems.at[7])
    ing_out.start()
    wire.drain()
    assert wire.count <= N_SEMS, wire.count
    for out in (gd_out, gu_out, mix_out, ing_out):
        out.wait()


def hand_over(*refs):
    sems = refs[-1]
    copies = [pltpu.make_async_copy(refs[i], refs[4 + i], sems.at[i]) for i in range(4)]
    for c in copies:
        c.start()
    for c in copies:
        c.wait()


def local(tokens, w_up, w_down, cotangent):
    scratch = [pltpu.VMEM(shape, dtype) for shape, dtype in SCRATCH.values()]
    scratch += [pltpu.SemaphoreType.DMA((N_SEMS,)), pltpu.SemaphoreType.DMA((N_SEMS,))]
    scratch += [pltpu.SemaphoreType.DMA((8,))]
    outs = (
        jax.ShapeDtypeStruct(tokens.shape, BF),
        jax.ShapeDtypeStruct(cotangent.shape, BF),
        jax.ShapeDtypeStruct(w_up.shape, BF),
        jax.ShapeDtypeStruct(w_down.shape, BF),
    )
    tokens, w_up, w_down, cotangent = (
        pltpu.with_memory_space_constraint(a, pltpu.HBM)
        for a in (tokens, w_up, w_down, cotangent)
    )
    made = pl.pallas_call(
        kernel,
        out_shape=outs,
        in_specs=[pl.BlockSpec(memory_space=pltpu.HBM)] * 4,
        out_specs=[pl.BlockSpec(memory_space=pl.ANY)] * 4,
        scratch_shapes=scratch,
        compiler_params=pltpu.CompilerParams(
            collective_id=0, has_side_effects=True, vmem_limit_bytes=32 * 1024 * 1024
        ),
        name="block",
    )(tokens, w_up, w_down, cotangent)
    return pl.pallas_call(
        hand_over,
        out_shape=outs,
        in_specs=[pl.BlockSpec(memory_space=pl.ANY)] * 4,
        out_specs=[pl.BlockSpec(memory_space=pl.ANY)] * 4,
        scratch_shapes=[pltpu.SemaphoreType.DMA((4,))],
        compiler_params=pltpu.CompilerParams(vmem_limit_bytes=1024 * 1024),
        name="hand_over",
    )(*made)


def solution(mesh):
    return jax.shard_map(
        local,
        mesh=mesh,
        in_specs=(
            P("fsdp", "tcol"),
            P("tcol", ("fsdp", "trow")),
            P(("fsdp", "trow"), "tcol"),
            P("fsdp", "tcol"),
        ),
        out_specs=(
            P("fsdp", "tcol"),
            P("fsdp", "tcol"),
            P("tcol", ("fsdp", "trow")),
            P(("fsdp", "trow"), "tcol"),
        ),
        check_vma=False,
    )
```

profile of v0, /device:TPU:2, one launch (start us, length us, event | category | flops | bytes accessed | tf_op | source)
XLA Modules:
  0.0 99.9 jit_solution(12188801746033642202)
XLA Ops:
  0.6 98.1 %block.1 = (bf16[256,1024]{1,0:T(8,128)(2,1)S(1)}, bf16[256,1024]{1,0:T(8,128)(2,1)S(1)}, bf16[1024,128]{1,0:T(8,128)(2,1)S(1)}, bf16[128,1024]{1,0:T(8,128)(2,1)S(1)}) custom-call(bf16[256,1024]{1,0:T(8,128)(2,1)} %tok_h.1, bf16[1024,128]{1,0:T(8,128)(2,1)} %wu_h.1, bf16[128,1024]{1,0:T(8,128)(2,1)} %wd_h.1, bf16[256,1024]{1,0:T(8,128)(2,1)} %cot_h.1), custom_call_target="tpu_custom_call" | custom-call | tf_op jit(solution)/shard_map/block/pallas_call | solution.py:707
  98.8 1.2 %hand_over.1 = (bf16[256,1024]{1,0:T(8,128)(2,1)}, bf16[256,1024]{1,0:T(8,128)(2,1)}, bf16[1024,128]{1,0:T(8,128)(2,1)}, bf16[128,1024]{1,0:T(8,128)(2,1)}) custom-call(bf16[256,1024]{1,0:T(8,128)(2,1)S(1)} %get-tuple-element.8.refs_0_, bf16[256,1024]{1,0:T(8,128)(2,1)S(1)} %get-tuple-element.9.refs_1_, bf16[1024,128]{1,0:T(8,128)(2,1)S(1)} %get-tuple-element.10.refs_2_, ...), custom_call_target="tpu_custom_call" | custom-call | tf_op jit(solution)/shard_map/hand_over/pallas_call | solution.py:718
where the time goes:
time: 100 us; the launch traced here: 99.9 us
  Pallas kernels  99.3 us (99%)
    pallas_call x1, Pallas kernels, local(): pl.pallas_call(kernel, out_shape=outs, in_specs=[pl.BlockSpec(memory_spac...  98.1 us

commit v1 on v0

--- a/solution.py
+++ b/solution.py
@@ -30,39 +30,54 @@
     def __init__(self, send_sems, recv_sems):
         self.send_sems, self.recv_sems = send_sems, recv_sems
         self.count = 0
-        self.sent = []
+        self.turn = 0
+        self.last = {}
 
     def slot(self):
         self.count += 1
         return self.count - 1
 
     def copy(self, src, dst, device, slot):
-        return pltpu.make_async_remote_copy(
+        turn = self.turn % N_SENDS
+        self.turn += 1
+        made = pltpu.make_async_remote_copy(
             src_ref=src,
             dst_ref=dst,
-            send_sem=self.send_sems.at[slot],
+            send_sem=self.send_sems.at[turn],
             recv_sem=self.recv_sems.at[slot],
             device_id=device,
             device_id_type=pl.DeviceIdType.MESH,
         )
-
-    def send(self, src, dst, device, slot=None, when=None):
-        slot = self.slot() if slot is None else slot
-        made = self.copy(src, dst, device, slot)
-        if when is None:
-            made.start()
-        else:
-            pl.when(when)(made.start)
-        self.sent.append((made, when))
-        return made
-
-    def drain(self):
-        for made, when in self.sent:
+        self.finish(turn)
+        return made, turn
+
+    def finish(self, turn):
+        if turn in self.last:
+            made, when = self.last.pop(turn)
             if when is None:
                 made.wait_send()
             else:
                 pl.when(when)(made.wait_send)
 
+    def started(self, pair, when=None):
+        self.last[pair[1]] = (pair[0], when)
+
+    def send(self, src, dst, device, slot=None, when=None):
+        pair = self.copy(src, dst, device, self.slot() if slot is None else slot)
+        if when is None:
+            pair[0].start()
+        else:
+            pl.when(when)(pair[0].start)
+        self.started(pair, when)
+        return pair[0]
+
+    def wait_for(self, ref, slot):
+        pltpu.make_async_copy(ref, ref, self.recv_sems.at[slot]).wait()
+
+    def drain(self):
+        for turn in list(self.last):
+            self.finish(turn)
+
 
 class RingSum:
     def __init__(self, wire, plus, minus, block, half, bufs):
@@ -80,21 +95,22 @@
 
     def start_near(self):
         w, half = self.w, self.half
-        self.c3 = w.send(self.block(1, 1), half(self.r2p, 1), self.plus)
-        self.c4 = w.send(self.block(-1, 0), half(self.r2m, 0), self.minus)
+        self.sp, self.sm = w.slot(), w.slot()
+        w.send(self.block(1, 1), half(self.r2p, 1), self.plus, self.sp)
+        w.send(self.block(-1, 0), half(self.r2m, 0), self.minus, self.sm)
 
     def mid(self):
         w, half = self.w, self.half
         self.c1.wait_recv()
         self.ga[...] = (self.block(1, 0)[...].astype(F32) + self.r1a[...].astype(F32)).astype(BF)
-        self.c5 = w.send(self.ga, half(self.r2p, 0), self.plus)
+        w.send(self.ga, half(self.r2p, 0), self.plus, self.sp)
         self.c2.wait_recv()
         self.gb[...] = (self.block(-1, 1)[...].astype(F32) + self.r1b[...].astype(F32)).astype(BF)
-        self.c6 = w.send(self.gb, half(self.r2m, 1), self.minus)
+        w.send(self.gb, half(self.r2m, 1), self.minus, self.sm)
 
     def end(self, own):
-        for c in (self.c3, self.c4, self.c5, self.c6):
-            c.wait_recv()
+        self.w.wait_for(self.r2p, self.sp)
+        self.w.wait_for(self.r2m, self.sm)
         return own + self.r2p[...].astype(F32) + self.r2m[...].astype(F32)
 
 
@@ -126,23 +142,46 @@
         self.f1.wait_recv()
 
 
+class BlockCopy:
+    def __init__(self, wire, plus, minus, view, whole):
+        self.w, self.plus, self.minus, self.view, self.whole = wire, plus, minus, view, whole
+
+    def start(self):
+        w, mine = self.w, self.whole(0)
+        self.p = w.send(mine, mine, self.plus)
+        self.m = w.send(mine, mine, self.minus)
+        self.slot = w.slot()
+
+    def mid(self):
+        w = self.w
+        self.p.wait_recv()
+        half = self.view(-1, 0)
+        w.send(half, half, self.plus, self.slot)
+        self.m.wait_recv()
+        half = self.view(1, 1)
+        w.send(half, half, self.minus, self.slot)
+
+    def end(self):
+        self.w.wait_for(self.whole(2), self.slot)
+
+
 SCRATCH = dict(
     x=((512, 1024), BF),
     c=((512, 1024), BF),
     tk=((256, 1024), BF),
-    wu=((1024, 512), BF),
+    wu=((4, 1024, 128), BF),
     wd=((512, 1024), BF),
     sstat=((8, 256), F32),
     rstat=((3, 8, 256), F32),
     mean=((256, 128), F32),
     rstd=((256, 128), F32),
-    part=((2, 512, 512), BF),
+    part=((2, 4, 512, 128), BF),
     pa=((2, 4, 256, 128), BF),
     pb=((2, 4, 256, 128), BF),
     pf=((2, 4, 256, 128), BF),
     pg=((2, 4, 256, 128), BF),
     pre=((4, 256, 128), F32),
-    hid=((2, 512, 512), BF),
+    hid=((2, 4, 512, 128), BF),
     bs=((2, 256, 1024), BF),
     br=((2, 256, 1024), BF),
     xacc=((2, 256, 1024), F32),
@@ -163,7 +202,8 @@
     zgb=((2, 16, 512), BF),
     fin=((2, 256, 1024), BF),
     ts=((1, 128), F32),
-    tr=((15, 1, 128), F32),
+    tr=((3, 1, 128), F32),
+    tz=((4, 1, 128), F32),
     gdp=((512, 1024), BF),
     gdo=((128, 1024), F32),
     gd1a=((64, 1024), BF),
@@ -173,7 +213,7 @@
     gdga=((64, 1024), BF),
     gdgb=((64, 1024), BF),
     gdout=((128, 1024), BF),
-    gup=((1024, 512), BF),
+    gup=((4, 1024, 128), BF),
     guo=((1024, 128), F32),
     gu1a=((512, 128), BF),
     gu1b=((512, 128), BF),
@@ -183,7 +223,8 @@
     gugb=((512, 128), BF),
     guout=((1024, 128), BF),
 )
-N_SEMS = 224
+N_SEMS = 149
+N_SENDS = 32
 
 
 def rows_of(index, size):
@@ -216,22 +257,20 @@
     right = zl // 2
     mate = zl + 1 - 2 * lax.rem(zl, 2)
     far_hub = 2 - right
+    far_end = 3 - 3 * right
     is_hub = jnp.logical_or(zl == 1, zl == 2)
     is_end = jnp.logical_or(zl == 0, zl == 3)
 
     barrier = pltpu.get_barrier_semaphore()
-    others = [partner, y_plus, y_minus, x_plus, x_minus]
-    for dz in range(4):
-        for dl in range(4):
-            if dz or dl:
-                fs, tr, _ = at(dzh=dz)
-                others.append((fs, tr, lax.rem(zl + dl, 4)))
+    z_plus, z_minus = at(dzh=1), at(dzh=3)
+    others = [partner, y_plus, y_minus, x_plus, x_minus, z_plus, z_minus]
+    others += [at_zl(lax.rem(zl + k, 4)) for k in (1, 2, 3)]
     loads = [
         pltpu.make_async_copy(src, dst, local_sems.at[i])
         for i, (src, dst) in enumerate(
             (
                 (tok_h, s["tk"]),
-                (wu_h, s["wu"].at[:, 0:128]),
+                (wu_h, s["wu"].at[0]),
                 (wd_h, s["wd"].at[0:128]),
                 (cot_h, s["c"].at[0:256]),
             )
@@ -256,7 +295,7 @@
     pl.semaphore_wait(barrier, len(others))
 
     def wu_at(pos, h):
-        return s["wu"].at[h * 512 : (h + 1) * 512, pos * 128 : (pos + 1) * 128]
+        return s["wu"].at[pos, h * 512 : (h + 1) * 512]
 
     def wd_at(pos, h):
         return s["wd"].at[pos * 128 + h * 64 : pos * 128 + (h + 1) * 64]
@@ -275,45 +314,56 @@
 
     ups, downs = weights(wu_at), weights(wd_at)
     ups.start()
-    stat_copies = [
-        wire.send(s["sstat"], s["rstat"].at[k - 1], at_zl(lax.rem(zl + k, 4))) for k in (1, 2, 3)
-    ]
+    stat_slot = wire.slot()
+    for k in (1, 2, 3):
+        wire.send(s["sstat"], s["rstat"].at[k - 1], at_zl(lax.rem(zl + k, 4)), stat_slot)
     cot_copy = wire.send(s["c"].at[0:256], s["c"].at[256:512], partner)
 
     class Exchange:
         def __init__(self, which, pos, first, count):
             self.which, self.first, self.count = which, first, count
-            self.lanes = slice(pos * 128, (pos + 1) * 128)
+            self.pos = pos
             self.i = (which, pos, slice(first, first + count))
             self.slots = [wire.slot() for _ in range(6)]
 
         def rows(self, side):
+            if isinstance(side, int):
+                return pl.ds(side * 256 + self.first, self.count)
             return pl.ds(pl.multiple_of(side * 256 + self.first, 128), self.count)
 
         def part(self, side):
-            return s["part"].at[self.which, self.rows(side), self.lanes]
+            return s["part"].at[self.which, self.pos, self.rows(side)]
 
         def back(self, side):
-            return s["hid"].at[self.which, self.rows(side), self.lanes]
+            return s["hid"].at[self.which, self.pos, self.rows(side)]
 
         def start(self):
-            far, near = self.slots[0:2]
-            to = at_zl(mate)
-            self.far = wire.send(self.part(1 - right), s["pb"].at[self.i], to, far, is_end)
-            self.near = wire.send(self.part(right), s["pa"].at[self.i], to, near, is_end)
+            self.far = wire.send(
+                self.part(1 - right), s["pb"].at[self.i], at_zl(mate), self.slots[0], is_end
+            )
+
+        def start_side(self, side):
+            to, part, (far, near) = at_zl(mate), self.part(side), self.slots[0:2]
+            self.near = wire.send(part, s["pa"].at[self.i], to, near, zl == 3 * side)
+            self.far = wire.send(part, s["pb"].at[self.i], to, far, zl == 3 - 3 * side)
+
+        def start_near(self):
+            self.near = wire.send(
+                self.part(right), s["pa"].at[self.i], at_zl(mate), self.slots[1], is_end
+            )
 
         def mid(self):
-            made = wire.copy(s["pg"].at[self.i], s["pf"].at[self.i], at_zl(far_hub), self.slots[2])
+            pair = wire.copy(s["pg"].at[self.i], s["pf"].at[self.i], at_zl(far_hub), self.slots[2])
 
             @pl.when(is_hub)
             def _():
                 self.far.wait_recv()
                 both = self.part(1 - right)[...].astype(F32) + s["pb"][self.i].astype(F32)
                 s["pg"][self.i] = both.astype(BF)
-                made.start()
-
-            wire.sent.append((made, is_hub))
-            self.cross = made
+                pair[0].start()
+
+            wire.started(pair, is_hub)
+            self.cross = pair[0]
 
         def end(self, finish):
             mine = self.back(right)
@@ -326,24 +376,25 @@
                 self.cross.wait_recv()
                 total = self.part(right)[...].astype(F32) + s["pa"][self.i].astype(F32)
                 total = total + s["pf"][self.i].astype(F32)
-                s["hid"][self.which, self.rows(right), self.lanes] = finish(total, self.i)
-                across.start()
-                down.start()
-
-            wire.sent += [(across, is_hub), (down, is_hub)]
-            self.across, self.down = across, down
+                s["hid"][self.which, self.pos, self.rows(right)] = finish(total, self.i)
+                across[0].start()
+                down[0].start()
+
+            wire.started(across, is_hub)
+            wire.started(down, is_hub)
+            self.across, self.down = across[0], down[0]
 
         def back_mid(self):
             theirs = self.back(1 - right)
-            made = wire.copy(theirs, theirs, at_zl(mate), self.slots[5])
+            pair = wire.copy(theirs, theirs, at_zl(mate), self.slots[5])
 
             @pl.when(is_hub)
             def _():
                 self.across.wait_recv()
-                made.start()
-
-            wire.sent.append((made, is_hub))
-            self.passed = made
+                pair[0].start()
+
+            wire.started(pair, is_hub)
+            self.passed = pair[0]
 
         def back_end(self):
             @pl.when(is_end)
@@ -351,6 +402,31 @@
                 self.down.wait_recv()
                 self.passed.wait_recv()
 
+    class LastExchange(Exchange):
+        def end(self, finish):
+            mine = self.back(right)
+            beyond = wire.copy(mine, mine, at_zl(far_end), self.slots[5])
+            across = wire.copy(mine, mine, at_zl(far_hub), self.slots[3])
+            down = wire.copy(mine, mine, at_zl(mate), self.slots[4])
+
+            @pl.when(is_hub)
+            def _():
+                self.near.wait_recv()
+                self.cross.wait_recv()
+                total = self.part(right)[...].astype(F32) + s["pa"][self.i].astype(F32)
+                total = total + s["pf"][self.i].astype(F32)
+                s["hid"][self.which, self.pos, self.rows(right)] = finish(total, self.i)
+                beyond[0].start()
+                across[0].start()
+                down[0].start()
+
+            for pair in (beyond, across, down):
+                wire.started(pair, is_hub)
+            self.passed, self.across, self.down = beyond[0], across[0], down[0]
+
+        def back_mid(self):
+            pl.when(is_hub)(self.across.wait_recv)
+
     def gelu_of(total, i):
         s["pre"][i[1:]] = total
         return gelu_value(total).astype(BF)
@@ -360,23 +436,33 @@
 
     pres = [[Exchange(0, pos, 0, 256)] for pos in range(4)]
     dhs = [[Exchange(1, pos, 0, 256)] for pos in range(3)]
-    dhs.append([Exchange(1, 3, 0, 128), Exchange(1, 3, 128, 128)])
+    dhs.append([LastExchange(1, 3, 0, 128), LastExchange(1, 3, 128, 128)])
 
     def every(exchanges, step, *args):
         for e in exchanges:
             getattr(e, step)(*args)
 
+    def side_by_side(blocks):
+        return blocks[0] if len(blocks) == 1 else jnp.concatenate(blocks, axis=1)
+
+    def put_part(which, first, last, value):
+        for pos in range(first, last):
+            lanes = slice((pos - first) * 128, (pos - first + 1) * 128)
+            s["part"][which, pos] = value[:, lanes].astype(BF)
+
     def pre_part(first, last):
-        lanes = slice(first * 128, last * 128)
-        s["part"][0, :, lanes] = dot(s["x"][...], s["wu"][:, lanes], 1, 0).astype(BF)
-        for pos in range(first, last):
-            every(pres[pos], "start")
+        blocks = side_by_side([s["wu"][pos] for pos in range(first, last)])
+        put_part(0, first, last, dot(s["x"][...], blocks, 1, 0))
+        for step in ("start", "start_near"):
+            for pos in range(first, last):
+                every(pres[pos], step)
 
     def dh_part(first, last):
         lanes = slice(first * 128, last * 128)
-        s["part"][1, :, lanes] = dot(s["c"][...], s["wd"][lanes], 1, 1).astype(BF)
-        for pos in range(first, last):
-            every(dhs[pos], "start")
+        put_part(1, first, last, dot(s["c"][...], s["wd"][lanes], 1, 1))
+        for step in ("start", "start_near"):
+            for pos in range(first, last):
+                every(dhs[pos], step)
 
     def pre_done(pos):
         every(pres[pos], "end", gelu_of)
@@ -384,11 +470,15 @@
     def dh_done(pos):
         every(dhs[pos], "end", dpre_of)
 
+    def own_block(which, side, value):
+        s["part"][which, 0, side * 256 : (side + 1) * 256] = value.astype(BF)
+        every((pres, dhs)[which][0], "start_side", side)
+
+    own_block(1, 0, dot(s["c"][0:256], s["wd"][0:128], 1, 1))
     cot_copy.wait_recv()
-    dh_part(0, 1)
-
-    for c in stat_copies:
-        c.wait_recv()
+    own_block(1, 1, dot(s["c"][256:512], s["wd"][0:128], 1, 1))
+
+    wire.wait_for(s["rstat"], stat_slot)
     total = s["sstat"][...] + s["rstat"][0] + s["rstat"][1] + s["rstat"][2]
     total = jnp.transpose(jnp.concatenate([total, jnp.zeros((120, 256), F32)], axis=0))
     mean = total[:, 0:1] / 4096.0
@@ -398,10 +488,11 @@
     s["rstd"][...] = jnp.broadcast_to(rstd, (256, 128))
     s["x"][0:256] = ((s["tk"][...].astype(F32) - mean) * rstd).astype(BF)
     x_copy = wire.send(s["x"].at[0:256], s["x"].at[256:512], partner)
+    own_block(0, 0, dot(s["x"][0:256], s["wu"][0], 1, 0))
     ups.mid()
     downs.start()
     x_copy.wait_recv()
-    pre_part(0, 1)
+    own_block(0, 1, dot(s["x"][256:512], s["wu"][0], 1, 0))
     every(dhs[0], "mid")
     ups.near_end()
     pre_part(1, 3)
@@ -416,22 +507,22 @@
     every(pres[3], "mid")
     every(pres[0], "back_mid")
     every(dhs[0], "back_mid")
-    pre_done(1)
     downs.near_end()
     dh_part(1, 3)
+    pre_done(1)
     pre_done(2)
-    every(pres[1], "back_mid")
-    pre_done(3)
+    every(dhs[1], "mid")
     downs.far_end()
     dh_part(3, 4)
-    every(dhs[1], "mid")
     every(dhs[2], "mid")
+    pre_done(3)
+    every(pres[1], "back_mid")
     every(pres[2], "back_mid")
+    dh_done(1)
+    every(pres[3], "back_mid")
     every(dhs[3], "mid")
-    every(pres[3], "back_mid")
-    dh_done(1)
     dh_done(2)
-    dh_done(3)
+    every(dhs[1], "back_mid")
 
     def rows(rel_x, rel_z):
         first = lax.rem(xx + rel_x, 4) * 64 + lax.rem(zh + rel_z, 4) * 16
@@ -528,16 +619,10 @@
         def view(rel, h):
             return s["fin"].at[o, rows(rel % 4, rel_z % 4), h * 512 : (h + 1) * 512]
 
-        return RingCopy(
-            wire,
-            x_plus,
-            x_minus,
-            own=lambda h: view(0, h),
-            at_plus=lambda h: view(0, h),
-            at_minus=lambda h: view(0, h),
-            near=view,
-            far=view,
-        )
+        def whole(rel):
+            return s["fin"].at[o, rows(rel % 4, rel_z % 4)]
+
+        return BlockCopy(wire, x_plus, x_minus, view, whole)
 
     def back_x_start(o, rel_z):
         spread = back_x(o, rel_z)
@@ -552,7 +637,7 @@
 
     def gu_block(rel, h):
         pos = pos_of[rel]
-        return s["gup"].at[h * 512 : (h + 1) * 512, pos * 128 : (pos + 1) * 128]
+        return s["gup"].at[pos, h * 512 : (h + 1) * 512]
 
     gd_names = ("gd1a", "gd1b", "gd2p", "gd2m", "gdga", "gdgb")
     gu_names = ("gu1a", "gu1b", "gu2p", "gu2m", "guga", "gugb")
@@ -565,39 +650,51 @@
         [s[n] for n in gu_names],
     )
 
+    def hid(which, first, last):
+        return side_by_side([s["hid"][which, pos, first:last] for pos in range(4)])
+
     for pos in range(4):
         every(pres[pos], "back_end")
     branch_copy = out_part(
-        0, lambda half: dot(s["hid"][0, half * 256 : (half + 1) * 256], s["wd"][...], 1, 0)
+        0, lambda half: dot(hid(0, half * 256, half * 256 + 256), s["wd"][...], 1, 0)
     )
-    every(dhs[1], "back_mid")
+    dh_done(3)
     every(dhs[2], "back_mid")
-    every(dhs[3], "back_mid")
     x_start(0, branch_copy)
-    grad = dot(s["hid"][0], s["c"][...], 0, 0)
+    grad = dot(hid(0, 0, 512), s["c"][...], 0, 0)
     s["gdo"][...] = grad[0:128]
     s["gdp"][128:512] = grad[128:512].astype(BF)
     gd_sum.start()
+    every(dhs[3], "back_mid")
+    x_sums[0][0].mid()
+    x_sums[0][1].mid()
     for pos in range(4):
         every(dhs[pos], "back_end")
 
     dnorm_copy = out_part(
-        1, lambda half: dot(s["hid"][1, half * 256 : (half + 1) * 256], s["wu"][...], 1, 1)
+        1,
+        lambda half: dot(
+            hid(1, half * 256, half * 256 + 256),
+            side_by_side([s["wu"][pos] for pos in range(4)]),
+            1,
+            1,
+        ),
     )
-    x_sums[0][0].mid()
-    x_sums[0][1].mid()
+    z_start(0, 0)
     x_start(1, dnorm_copy)
-    grad = dot(s["x"][...], s["hid"][1], 0, 0)
+    z_start(0, 1)
+    grad = dot(s["x"][...], hid(1, 0, 512), 0, 0)
     s["guo"][...] = grad[:, 0:128]
-    s["gup"][:, 128:512] = grad[:, 128:512].astype(BF)
+    for pos in (1, 2, 3):
+        s["gup"][pos] = grad[:, pos * 128 : (pos + 1) * 128].astype(BF)
     gu_sum.start()
-    z_start(0, 0)
-    z_start(0, 1)
     x_sums[1][0].mid()
     x_sums[1][1].mid()
     gd_sum.mid()
     z_start(1, 0)
     z_start(1, 1)
+
+    z_sums[0].mid()
 
     lane = lax.broadcasted_iota(jnp.int32, (16, 128), 1)
     row = lax.broadcasted_iota(jnp.int32, (16, 128), 0)
@@ -612,15 +709,15 @@
         spot = jnp.where(lane == place, first, jnp.where(lane == place + 64, second, 0.0))
         line = line + jnp.sum(spot, axis=0, keepdims=True)
     s["ts"][...] = line
-    moment_copies = []
-    for dz in range(4):
-        for dl in range(4):
-            if dz or dl:
-                fs, tr, _ = at(dzh=dz)
-                other = (fs, tr, lax.rem(zl + dl, 4))
-                moment_copies.append(wire.send(s["ts"], s["tr"].at[dz * 4 + dl - 1], other))
-    z_sums[0].mid()
+    moment_slot = wire.slot()
+    for k in (1, 2, 3):
+        wire.send(s["ts"], s["tr"].at[k - 1], at_zl(lax.rem(zl + k, 4)), moment_slot)
     gu_sum.mid()
+    wire.wait_for(s["tr"], moment_slot)
+    s["tz"][0] = s["ts"][...] + s["tr"][0] + s["tr"][1] + s["tr"][2]
+    moment_copies = [
+        wire.send(s["tz"].at[0], s["tz"].at[d], at(dzh=d)) for d in (2, 1, 3)
+    ]
     z_sums[1].mid()
     s["fin"][0, mine, :] = (s["tk"][mine, :].astype(F32) + z_done(0)).astype(BF)
     z_back0 = back_z(0)
@@ -632,9 +729,7 @@
     dnorm = z_done(1)
     for c in moment_copies:
         c.wait_recv()
-    line = s["ts"][...]
-    for k in range(15):
-        line = line + s["tr"][k]
+    line = s["tz"][0] + s["tz"][1] + s["tz"][2] + s["tz"][3]
     place = row + zh * 16
     moment_one = jnp.sum(jnp.where(lane == place, line, 0.0), axis=1, keepdims=True) / 4096.0
     moment_two = jnp.sum(jnp.where(lane == place + 64, line, 0.0), axis=1, keepdims=True) / 4096.0
@@ -644,39 +739,37 @@
     s["fin"][1, mine, :] = grad.astype(BF)
     z_back1 = back_z(1)
     x_backs1 = [back_x_start(1, 0)]
+    x_backs0[0].mid()
     z_back0.mid()
     z_back0.near_end()
     x_backs0 += [back_x_start(0, 1), back_x_start(0, 3)]
-    x_backs0[0].mid()
     x_backs1[0].mid()
-    z_back1.mid()
-    z_back1.near_end()
-    x_backs1 += [back_x_start(1, 1), back_x_start(1, 3)]
     x_backs0[1].mid()
     x_backs0[2].mid()
     z_back0.far_end()
     x_backs0.append(back_x_start(0, 2))
-    x_backs1[1].mid()
-    x_backs1[2].mid()
+    z_back1.mid()
+    z_back1.near_end()
+    x_backs1 += [back_x_start(1, 1), back_x_start(1, 3)]
     s["guout"][...] = gu_sum.end(s["guo"][...]).astype(BF)
     gu_out = pltpu.make_async_copy(s["guout"], gu_h, local_sems.at[5])
     gu_out.start()
+    x_backs1[1].mid()
+    x_backs1[2].mid()
     x_backs0[3].mid()
     z_back1.far_end()
     x_backs1.append(back_x_start(1, 2))
     for spread in x_backs0:
-        spread.near_end()
-        spread.far_end()
+        spread.end()
     mix_out = pltpu.make_async_copy(s["fin"].at[0], mix_h, local_sems.at[6])
     mix_out.start()
     x_backs1[3].mid()
     for spread in x_backs1:
-        spread.near_end()
-        spread.far_end()
+        spread.end()
     ing_out = pltpu.make_async_copy(s["fin"].at[1], ing_h, local_sems.at[7])
     ing_out.start()
     wire.drain()
-    assert wire.count <= N_SEMS, wire.count
+    assert wire.count == N_SEMS, wire.count
     for out in (gd_out, gu_out, mix_out, ing_out):
         out.wait()
 
@@ -692,7 +785,7 @@
 
 def local(tokens, w_up, w_down, cotangent):
     scratch = [pltpu.VMEM(shape, dtype) for shape, dtype in SCRATCH.values()]
-    scratch += [pltpu.SemaphoreType.DMA((N_SEMS,)), pltpu.SemaphoreType.DMA((N_SEMS,))]
+    scratch += [pltpu.SemaphoreType.DMA((N_SENDS,)), pltpu.SemaphoreType.DMA((N_SEMS,))]
     scratch += [pltpu.SemaphoreType.DMA((8,))]
     outs = (
         jax.ShapeDtypeStruct(tokens.shape, BF),

time: 100 us -> 97 us (0.970)
  the two profiles are of different devices: /device:TPU:2 before, /device:TPU:4 now
where the time goes in v1:
time: 97 us; the launch traced here: 96.8 us
  Pallas kernels  96.2 us (99%)
    pallas_call x1, Pallas kernels, local(): pl.pallas_call(kernel, out_shape=outs, in_specs=[pl.BlockSpec(memory_spac...  95 us

profile of v1, /device:TPU:4, one launch (start us, length us, event | category | flops | bytes accessed | tf_op | source)
XLA Modules:
  0.0 96.8 jit_solution(13715549840630685056)
XLA Ops:
  0.6 95.0 %block.1 = (bf16[256,1024]{1,0:T(8,128)(2,1)S(1)}, bf16[256,1024]{1,0:T(8,128)(2,1)S(1)}, bf16[1024,128]{1,0:T(8,128)(2,1)S(1)}, bf16[128,1024]{1,0:T(8,128)(2,1)S(1)}) custom-call(bf16[256,1024]{1,0:T(8,128)(2,1)} %tok_h.1, bf16[1024,128]{1,0:T(8,128)(2,1)} %wu_h.1, bf16[128,1024]{1,0:T(8,128)(2,1)} %wd_h.1, bf16[256,1024]{1,0:T(8,128)(2,1)} %cot_h.1), custom_call_target="tpu_custom_call" | custom-call | tf_op jit(solution)/shard_map/block/pallas_call | solution.py:800
  95.6 1.2 %hand_over.1 = (bf16[256,1024]{1,0:T(8,128)(2,1)}, bf16[256,1024]{1,0:T(8,128)(2,1)}, bf16[1024,128]{1,0:T(8,128)(2,1)}, bf16[128,1024]{1,0:T(8,128)(2,1)}) custom-call(bf16[256,1024]{1,0:T(8,128)(2,1)S(1)} %get-tuple-element.8.refs_0_, bf16[256,1024]{1,0:T(8,128)(2,1)S(1)} %get-tuple-element.9.refs_1_, bf16[1024,128]{1,0:T(8,128)(2,1)S(1)} %get-tuple-element.10.refs_2_, ...), custom_call_target="tpu_custom_call" | custom-call | tf_op jit(solution)/shard_map/hand_over/pallas_call | solution.py:811

commit v2 on v1

--- a/solution.py
+++ b/solution.py
@@ -666,8 +666,6 @@
     s["gdp"][128:512] = grad[128:512].astype(BF)
     gd_sum.start()
     every(dhs[3], "back_mid")
-    x_sums[0][0].mid()
-    x_sums[0][1].mid()
     for pos in range(4):
         every(dhs[pos], "back_end")
 
@@ -680,14 +678,16 @@
             1,
         ),
     )
-    z_start(0, 0)
+    x_sums[0][0].mid()
+    x_sums[0][1].mid()
     x_start(1, dnorm_copy)
-    z_start(0, 1)
     grad = dot(s["x"][...], hid(1, 0, 512), 0, 0)
     s["guo"][...] = grad[:, 0:128]
     for pos in (1, 2, 3):
         s["gup"][pos] = grad[:, pos * 128 : (pos + 1) * 128].astype(BF)
     gu_sum.start()
+    z_start(0, 0)
+    z_start(0, 1)
     x_sums[1][0].mid()
     x_sums[1][1].mid()
     gd_sum.mid()

time: 97 us -> 96.5 us (level)
  the two profiles are of different devices: /device:TPU:4 before, /device:TPU:16 now
where the time goes in v2:
time: 96.5 us; the launch traced here: 96.3 us
  Pallas kernels  95.7 us (99%)
    pallas_call x1, Pallas kernels, local(): pl.pallas_call(kernel, out_shape=outs, in_specs=[pl.BlockSpec(memory_spac...  94.5 us

profile of v2, /device:TPU:16, one launch (start us, length us, event | category | flops | bytes accessed | tf_op | source)
XLA Modules:
  0.0 96.3 jit_solution(557391294710908176)
XLA Ops:
  0.6 94.5 %block.1 = (bf16[256,1024]{1,0:T(8,128)(2,1)S(1)}, bf16[256,1024]{1,0:T(8,128)(2,1)S(1)}, bf16[1024,128]{1,0:T(8,128)(2,1)S(1)}, bf16[128,1024]{1,0:T(8,128)(2,1)S(1)}) custom-call(bf16[256,1024]{1,0:T(8,128)(2,1)} %tok_h.1, bf16[1024,128]{1,0:T(8,128)(2,1)} %wu_h.1, bf16[128,1024]{1,0:T(8,128)(2,1)} %wd_h.1, bf16[256,1024]{1,0:T(8,128)(2,1)} %cot_h.1), custom_call_target="tpu_custom_call" | custom-call | tf_op jit(solution)/shard_map/block/pallas_call | solution.py:800
  95.2 1.2 %hand_over.1 = (bf16[256,1024]{1,0:T(8,128)(2,1)}, bf16[256,1024]{1,0:T(8,128)(2,1)}, bf16[1024,128]{1,0:T(8,128)(2,1)}, bf16[128,1024]{1,0:T(8,128)(2,1)}) custom-call(bf16[256,1024]{1,0:T(8,128)(2,1)S(1)} %get-tuple-element.8.refs_0_, bf16[256,1024]{1,0:T(8,128)(2,1)S(1)} %get-tuple-element.9.refs_1_, bf16[1024,128]{1,0:T(8,128)(2,1)S(1)} %get-tuple-element.10.refs_2_, ...), custom_call_target="tpu_custom_call" | custom-call | tf_op jit(solution)/shard_map/hand_over/pallas_call | solution.py:811
